TPU v7x, 512 devices: a whole 4x8x8 slice. The times are simulated.
512 devices in a mesh: row: 32 (over y, x), col: 16 (over z, core).
Axes of the slice: x: 4, y: 8, z: 8, core: 2. Of those that a mesh axis runs over, the one named last changes fastest.
Arguments:
- pair_factors: float32 [12288, 1024], P(('row', 'col')), may hold values from -0.09375 to 0.09375
- k_prev: float32 [12288, 12288], P('row', 'col'), as said below
- energies: float32 [12288], P('row'), may hold values from 0.3 to 2
Outputs:
- casida: float32 [12288, 12288], P('row', 'col')
- vectors: float32 [12288, 8], P('row')
- images: float32 [12288, 8], P('row')
- tridiagonal: float32 [2, 8], replicated
Inputs may be any that keep to these rules, and one draw needn't show every extreme that they name: k_prev is exactly symmetric.
All inputs are finite; a program needn't handle non-finite values.
Results may differ from a plain program's by a relative error of at most 0.0003.
Values sent between devices are 32-bit elements; how exact they have to be, the bound alone decides.
A program may use at most 64 MiB of HBM per device.

v0:
```python
import jax
import jax.numpy as jnp
from jax import lax
from jax.sharding import Mesh
from jax.sharding import PartitionSpec as P

N = 12288
PC = 8
ROW = ("row_0", "row_1")
ROW_COL = ("row_0", "row_1", "col")


def laid_out(pieces, dim):
    pieces = jnp.moveaxis(pieces, 0, dim)
    shape = pieces.shape
    return pieces.reshape(*shape[:dim], shape[dim] * shape[dim + 1], *shape[dim + 2 :])


def sent_to_all(value, axis):
    copies = jnp.broadcast_to(value, (lax.axis_size(axis), *value.shape))
    return lax.all_to_all(copies, axis, split_axis=0, concat_axis=0, tiled=True)


def gathered_copies(value, axis, dim):
    return laid_out(sent_to_all(value, axis), dim)


def spread(value, axes, root):
    value = jnp.where(lax.axis_index(axes) == root, value, jnp.zeros_like(value))
    for axis in axes:
        value = lax.psum(value, axis)
    return value


def picked(value, axis, root):
    return lax.dynamic_index_in_dim(lax.all_gather(value, axis), root, 0, keepdims=False)


def over_copies(value, axis):
    everything = sent_to_all(value, axis)
    return jnp.sum(everything, axis=0)


def packed_total(arrays, axis):
    flat, at, outs = (jnp.concatenate([a.reshape(-1) for a in arrays]), 0, [])
    so_far = over_copies(flat, axis)
    for a in arrays:
        outs.append(so_far[at : at + a.size].reshape(a.shape))
        at += a.size
    return tuple(outs)


def shards(pair_factors, k_prev, energies):
    rows_here, cols_here = k_prev.shape
    per_col = lax.axis_size(ROW) // lax.axis_size("col")
    row_index = lax.axis_index(ROW)
    col_index = lax.axis_index("col")
    left_rows = gathered_copies(pair_factors, "col", 0)
    right_parts = []
    for offset in range(per_col):
        right_parts.append(spread(left_rows, ROW, per_col * col_index + offset))
    right_rows = jnp.concatenate(right_parts, axis=0)
    total = lax.dot_general(
        left_rows,
        right_rows,
        (((1,), (1,)), ((), ())),
        precision=lax.Precision.HIGHEST,
        preferred_element_type=jnp.float32,
    )
    global_rows = row_index * rows_here + jnp.arange(rows_here, dtype=jnp.int32)
    global_cols = col_index * cols_here + jnp.arange(cols_here, dtype=jnp.int32)
    on_diagonal = global_rows[:, None] == global_cols[None, :]
    casida = 4.0 * (k_prev + total) + jnp.where(on_diagonal, energies[:, None], 0.0)
    col_ids = jnp.arange(PC, dtype=jnp.int32)
    scale = jnp.sqrt(jnp.float32(N))
    diag_list = []
    sub_list = []
    head_ids = jnp.arange(PC + 1, dtype=jnp.int32)
    upper = jnp.zeros((rows_here, PC), jnp.float32)
    lower = jnp.zeros((rows_here, PC), jnp.float32)
    upper_head = jnp.zeros((PC + 1, PC), jnp.float32)
    lower_head = jnp.zeros((PC + 1, PC), jnp.float32)
    on_first = row_index == 0
    for column_at in range(PC):
        raw_column = picked(casida[:, column_at], "col", 0)
        column = (
            raw_column
            - jnp.dot(upper, lower_head[column_at], precision=lax.Precision.HIGHEST)
            - jnp.dot(lower, upper_head[column_at], precision=lax.Precision.HIGHEST)
        )
        below = jnp.where(global_rows > column_at, column, 0.0)
        head_part = jnp.where(on_first, column[: PC + 1], 0.0)
        sigma, head, upper_proj, lower_proj = packed_total(
            (
                jnp.sum(below * below),
                head_part,
                jnp.dot(upper.T, below, precision=lax.Precision.HIGHEST),
                jnp.dot(lower.T, below, precision=lax.Precision.HIGHEST),
            ),
            ROW,
        )
        diag_list.append(head[column_at])
        lead = head[column_at + 1]
        root = jnp.sqrt(sigma)
        alpha = jnp.where(lead >= 0, -root, root)
        length = jnp.sqrt(jnp.maximum(2.0 * (sigma + jnp.abs(lead) * root), 1.0))
        unit = (below - alpha * (global_rows == column_at + 1).astype(jnp.float32)) / length
        unit_head = (
            jnp.where(head_ids > column_at, head, 0.0)
            - alpha * (head_ids == column_at + 1).astype(jnp.float32)
        ) / length
        upper_unit = (upper_proj - alpha * upper_head[column_at + 1]) / length
        lower_unit = (lower_proj - alpha * lower_head[column_at + 1]) / length
        partial_cols = jnp.dot(unit, casida, precision=lax.Precision.HIGHEST)
        summed_cols = over_copies(partial_cols, ROW)
        owner_block = picked(summed_cols, "col", row_index // per_col)
        image = lax.dynamic_slice_in_dim(owner_block, row_index % per_col * rows_here, rows_here, 0)
        image = (
            image
            - jnp.dot(upper, lower_unit, precision=lax.Precision.HIGHEST)
            - jnp.dot(lower, upper_unit, precision=lax.Precision.HIGHEST)
        )
        image = 2.0 * image
        image_head_part = jnp.where(on_first, image[: PC + 1], 0.0)
        product, image_head = packed_total((jnp.sum(image * unit), image_head_part), ROW)
        partner = image - product * unit
        partner_head = image_head - product * unit_head
        pick = (col_ids == column_at).astype(jnp.float32)[None, :]
        upper = upper + unit[:, None] * pick
        lower = lower + partner[:, None] * pick
        upper_head = upper_head + unit_head[:, None] * pick
        lower_head = lower_head + partner_head[:, None] * pick
        sub_list.append(alpha)
    tridiagonal = jnp.stack([jnp.stack(diag_list), jnp.stack(sub_list)])
    return (casida, scale * upper, scale * lower, tridiagonal)


def solution(mesh):
    split = Mesh(mesh.devices.reshape(8, 4, mesh.shape["col"]), ("row_0", "row_1", "col"))
    in_specs = (P(ROW_COL, None), P(ROW, "col"), P(ROW))
    out_specs = (P(ROW, "col"), P(ROW, None), P(ROW, None), P())
    return jax.shard_map(
        shards, mesh=split, in_specs=in_specs, out_specs=out_specs, check_vma=False
    )
```

profile of v0, /device:TPU:1, one launch (start us, length us, event | category | flops | bytes accessed | tf_op | source)
XLA Modules:
  0.0 898.8 jit_solution(7743463168844762544)
XLA Ops:
  7.2 2.2 broadcast_in_dim.166
  9.4 11.8 %all-to-all-start = ((f32[16,24,1024]{2,1,0:T(8,128)}), f32[16,24,1024]{2,1,0:T(8,128)S(1)}, u32[]{:S(2)}, u32[]{:S(2)}) async-start(f32[16,24,1024]{2,1,0:T(8,128)} %broadcast_in_dim.166), calls=%async_computation | async-start | bytes 3145728 | tf_op jit(solution)/shard_map/all_to_all | solution.py:21
  21.3 38.5 %all-to-all-done = f32[16,24,1024]{2,1,0:T(8,128)S(1)} async-done(((f32[16,24,1024]{2,1,0:T(8,128)}), f32[16,24,1024]{2,1,0:T(8,128)S(1)}, u32[]{:S(2)}, u32[]{:S(2)}) %all-to-all-start) | async-done | bytes 1572896 | tf_op jit(solution)/shard_map/all_to_all | solution.py:21
  61.8 93.9 %all-reduce.5.cloned.1.call-done = (f32[384,1024]{1,0:T(8,128)}, f32[384,1024]{1,0:T(8,128)}) async-done(((f32[384,1024]{1,0:T(8,128)}, f32[384,1024]{1,0:T(8,128)}), (f32[384,1024]{1,0:T(8,128)}, f32[384,1024]{1,0:T(8,128)})) %all-reduce.5.cloned.1.call-update) | async-done | bytes 3145744 | tf_op jit(solution)/shard_map/psum | solution.py:31
  159.1 85.0 %all-reduce.7.cloned.1.call-done = (f32[384,1024]{1,0:T(8,128)}, f32[384,1024]{1,0:T(8,128)}) async-done(((f32[384,1024]{1,0:T(8,128)}, f32[384,1024]{1,0:T(8,128)}), (f32[384,1024]{1,0:T(8,128)}, f32[384,1024]{1,0:T(8,128)})) %all-reduce.7.cloned.1.call-update) | async-done | bytes 3145744 | tf_op jit(solution)/shard_map/psum | solution.py:31
  244.1 7.3 fusion.13
  251.4 18.8 %all-gather = f32[6144,1]{0,1:T(1,128)S(1)} all-gather(f32[384,1]{0,1:T(1,128)S(1)} %get-tuple-element.93), channel_id=2, replica_groups=mesh['row_0'=8,'row_1'=4,'col'=16] {'col'}, dimensions={0}, use_global_device_ids=true | all-gather | bytes 26112 | tf_op jit(solution)/shard_map/all_gather | solution.py:36
  272.4 7.8 all-to-all-start.1
  280.3 8.5 all-to-all-done.1
  293.9 3.9 all-to-all-start.2
  297.7 16.2 %all-gather.1 = f32[6144,1]{0,1:T(1,128)S(1)} all-gather(f32[384,1]{0,1:T(1,128)S(1)} %get-tuple-element.92), channel_id=3, replica_groups=mesh['row_0'=8,'row_1'=4,'col'=16] {'col'}, dimensions={0}, use_global_device_ids=true | all-gather | bytes 26112 | tf_op jit(solution)/shard_map/all_gather | solution.py:36
  316.1 15.7 %all-gather.16 = f32[16,1,768]{2,1,0:T(1,128)S(1)} all-gather(f32[1,1,768]{2,1,0:T(1,128)S(1)} %reshape.407), channel_id=4, replica_groups=mesh['row_0'=8,'row_1'=4,'col'=16] {'col'}, dimensions={0}, use_global_device_ids=true | all-gather | bytes 52224 | tf_op jit(solution)/shard_map/all_gather | solution.py:36
  333.8 9.5 %all-to-all-start.3 = ((f32[32,1,10]{2,1,0:T(1,128)}), f32[32,1,10]{2,1,0:T(1,128)S(1)}, u32[]{:S(2)}, u32[]{:S(2)}) async-start(f32[32,1,10]{2,1,0:T(1,128)} %broadcast_in_dim.173), calls=%async_computation.3 | async-start | bytes 32768 | tf_op jit(solution)/shard_map/all_to_all | solution.py:21
  343.3 8.5 all-to-all-done.3
  355.0 3.8 all-to-all-start.4
  358.8 16.2 %all-gather.3 = f32[6144,1]{0,1:T(1,128)S(1)} all-gather(f32[384,1]{0,1:T(1,128)S(1)} %get-tuple-element.91), channel_id=5, replica_groups=mesh['row_0'=8,'row_1'=4,'col'=16] {'col'}, dimensions={0}, use_global_device_ids=true | all-gather | bytes 26112 | tf_op jit(solution)/shard_map/all_gather | solution.py:36
  380.1 9.7 %all-to-all-start.5 = ((f32[32,1,768]{2,1,0:T(1,128)}), f32[32,1,768]{2,1,0:T(1,128)S(1)}, u32[]{:S(2)}, u32[]{:S(2)}) async-start(f32[32,1,768]{2,1,0:T(1,128)} %broadcast_in_dim.175), calls=%async_computation.5 | async-start | bytes 196608 | tf_op jit(solution)/shard_map/all_to_all | solution.py:21
  390.3 8.6 all-to-all-done.5
  399.0 17.2 %all-gather.17 = f32[16,1,768]{2,1,0:T(1,128)S(1)} all-gather(f32[1,1,768]{2,1,0:T(1,128)S(1)} %reshape.409), channel_id=6, replica_groups=mesh['row_0'=8,'row_1'=4,'col'=16] {'col'}, dimensions={0}, use_global_device_ids=true | all-gather | bytes 52224 | tf_op jit(solution)/shard_map/all_gather | solution.py:36
  418.3 3.8 all-to-all-start.6
  422.1 8.5 all-to-all-done.6
  433.8 3.8 all-to-all-start.7
  437.7 15.9 %all-gather.5 = f32[6144,1]{0,1:T(1,128)S(1)} all-gather(f32[384,1]{0,1:T(1,128)S(1)} %get-tuple-element.90), channel_id=7, replica_groups=mesh['row_0'=8,'row_1'=4,'col'=16] {'col'}, dimensions={0}, use_global_device_ids=true | all-gather | bytes 26112 | tf_op jit(solution)/shard_map/all_gather | solution.py:36
  458.9 9.5 %all-to-all-start.8 = ((f32[32,1,768]{2,1,0:T(1,128)}), f32[32,1,768]{2,1,0:T(1,128)S(1)}, u32[]{:S(2)}, u32[]{:S(2)}) async-start(f32[32,1,768]{2,1,0:T(1,128)} %broadcast_in_dim.178), calls=%async_computation.8 | async-start | bytes 196608 | tf_op jit(solution)/shard_map/all_to_all | solution.py:21
  468.8 8.6 all-to-all-done.8
  477.5 17.2 %all-gather.18 = f32[16,1,768]{2,1,0:T(1,128)S(1)} all-gather(f32[1,1,768]{2,1,0:T(1,128)S(1)} %reshape.411), channel_id=8, replica_groups=mesh['row_0'=8,'row_1'=4,'col'=16] {'col'}, dimensions={0}, use_global_device_ids=true | all-gather | bytes 52224 | tf_op jit(solution)/shard_map/all_gather | solution.py:36
  496.8 3.8 all-to-all-start.9
  500.7 8.5 all-to-all-done.9
  512.4 3.8 all-to-all-start.10
  516.2 15.9 %all-gather.7 = f32[6144,1]{0,1:T(1,128)S(1)} all-gather(f32[384,1]{0,1:T(1,128)S(1)} %get-tuple-element.89), channel_id=9, replica_groups=mesh['row_0'=8,'row_1'=4,'col'=16] {'col'}, dimensions={0}, use_global_device_ids=true | all-gather | bytes 26112 | tf_op jit(solution)/shard_map/all_gather | solution.py:36
  537.4 9.5 %all-to-all-start.11 = ((f32[32,1,768]{2,1,0:T(1,128)}), f32[32,1,768]{2,1,0:T(1,128)S(1)}, u32[]{:S(2)}, u32[]{:S(2)}) async-start(f32[32,1,768]{2,1,0:T(1,128)} %broadcast_in_dim.181), calls=%async_computation.11 | async-start | bytes 196608 | tf_op jit(solution)/shard_map/all_to_all | solution.py:21
  547.4 8.6 all-to-all-done.11
  556.1 17.2 %all-gather.19 = f32[16,1,768]{2,1,0:T(1,128)S(1)} all-gather(f32[1,1,768]{2,1,0:T(1,128)S(1)} %reshape.413), channel_id=10, replica_groups=mesh['row_0'=8,'row_1'=4,'col'=16] {'col'}, dimensions={0}, use_global_device_ids=true | all-gather | bytes 52224 | tf_op jit(solution)/shard_map/all_gather | solution.py:36
  575.4 3.8 all-to-all-start.12
  579.2 8.5 all-to-all-done.12
  590.9 3.8 all-to-all-start.13
  594.8 15.9 %all-gather.9 = f32[6144,1]{0,1:T(1,128)S(1)} all-gather(f32[384,1]{0,1:T(1,128)S(1)} %get-tuple-element.88), channel_id=11, replica_groups=mesh['row_0'=8,'row_1'=4,'col'=16] {'col'}, dimensions={0}, use_global_device_ids=true | all-gather | bytes 26112 | tf_op jit(solution)/shard_map/all_gather | solution.py:36
  615.9 9.5 %all-to-all-start.14 = ((f32[32,1,768]{2,1,0:T(1,128)}), f32[32,1,768]{2,1,0:T(1,128)S(1)}, u32[]{:S(2)}, u32[]{:S(2)}) async-start(f32[32,1,768]{2,1,0:T(1,128)} %broadcast_in_dim.184), calls=%async_computation.14 | async-start | bytes 196608 | tf_op jit(solution)/shard_map/all_to_all | solution.py:21
  625.8 8.6 all-to-all-done.14
  634.5 17.2 %all-gather.20 = f32[16,1,768]{2,1,0:T(1,128)S(1)} all-gather(f32[1,1,768]{2,1,0:T(1,128)S(1)} %reshape.415), channel_id=12, replica_groups=mesh['row_0'=8,'row_1'=4,'col'=16] {'col'}, dimensions={0}, use_global_device_ids=true | all-gather | bytes 52224 | tf_op jit(solution)/shard_map/all_gather | solution.py:36
  653.8 3.8 all-to-all-start.15
  657.7 8.5 all-to-all-done.15
  669.4 4.0 all-to-all-start.16
  673.4 15.9 %all-gather.11 = f32[6144,1]{0,1:T(1,128)S(1)} all-gather(f32[384,1]{0,1:T(1,128)S(1)} %get-tuple-element.87), channel_id=13, replica_groups=mesh['row_0'=8,'row_1'=4,'col'=16] {'col'}, dimensions={0}, use_global_device_ids=true | all-gather | bytes 26112 | tf_op jit(solution)/shard_map/all_gather | solution.py:36
  694.5 9.5 %all-to-all-start.17 = ((f32[32,1,768]{2,1,0:T(1,128)}), f32[32,1,768]{2,1,0:T(1,128)S(1)}, u32[]{:S(2)}, u32[]{:S(2)}) async-start(f32[32,1,768]{2,1,0:T(1,128)} %broadcast_in_dim.187), calls=%async_computation.17 | async-start | bytes 196608 | tf_op jit(solution)/shard_map/all_to_all | solution.py:21
  704.5 8.6 all-to-all-done.17
  713.2 17.2 %all-gather.21 = f32[16,1,768]{2,1,0:T(1,128)S(1)} all-gather(f32[1,1,768]{2,1,0:T(1,128)S(1)} %reshape.417), channel_id=14, replica_groups=mesh['row_0'=8,'row_1'=4,'col'=16] {'col'}, dimensions={0}, use_global_device_ids=true | all-gather | bytes 52224 | tf_op jit(solution)/shard_map/all_gather | solution.py:36
  732.4 3.8 all-to-all-start.18
  736.3 8.5 all-to-all-done.18
  748.0 3.8 all-to-all-start.19
  751.9 15.9 %all-gather.13 = f32[6144,1]{0,1:T(1,128)S(1)} all-gather(f32[384,1]{0,1:T(1,128)S(1)} %get-tuple-element.86), channel_id=15, replica_groups=mesh['row_0'=8,'row_1'=4,'col'=16] {'col'}, dimensions={0}, use_global_device_ids=true | all-gather | bytes 26112 | tf_op jit(solution)/shard_map/all_gather | solution.py:36
  773.0 9.5 %all-to-all-start.20 = ((f32[32,1,768]{2,1,0:T(1,128)}), f32[32,1,768]{2,1,0:T(1,128)S(1)}, u32[]{:S(2)}, u32[]{:S(2)}) async-start(f32[32,1,768]{2,1,0:T(1,128)} %broadcast_in_dim.190), calls=%async_computation.20 | async-start | bytes 196608 | tf_op jit(solution)/shard_map/all_to_all | solution.py:21
  782.9 8.6 all-to-all-done.20
  791.6 17.2 %all-gather.22 = f32[16,1,768]{2,1,0:T(1,128)S(1)} all-gather(f32[1,1,768]{2,1,0:T(1,128)S(1)} %reshape.419), channel_id=16, replica_groups=mesh['row_0'=8,'row_1'=4,'col'=16] {'col'}, dimensions={0}, use_global_device_ids=true | all-gather | bytes 52224 | tf_op jit(solution)/shard_map/all_gather | solution.py:36
  810.9 3.8 all-to-all-start.21
  814.8 8.5 all-to-all-done.21
  826.6 3.8 all-to-all-start.22
  831.8 7.2 all-to-all-done.22
  844.4 3.9 all-to-all-start.23
  848.3 4.9 stack.39
  853.9 3.5 all-to-all-done.23
  857.5 18.1 %all-gather.23 = f32[16,1,768]{2,1,0:T(1,128)S(1)} all-gather(f32[1,1,768]{2,1,0:T(1,128)S(1)} %reshape.421), channel_id=17, replica_groups=mesh['row_0'=8,'row_1'=4,'col'=16] {'col'}, dimensions={0}, use_global_device_ids=true | all-gather | bytes 52224 | tf_op jit(solution)/shard_map/all_gather | solution.py:36
  877.7 4.9 all-to-all-start.24
  883.1 8.1 all-to-all-done.24
  (263 shorter events, 75.2 us)
Async XLA Ops:
  9.4 50.3 %all-to-all-start = ((f32[16,24,1024]{2,1,0:T(8,128)}), f32[16,24,1024]{2,1,0:T(8,128)S(1)}, u32[]{:S(2)}, u32[]{:S(2)}) async-start(f32[16,24,1024]{2,1,0:T(8,128)} %broadcast_in_dim.166), calls=%async_computation | async-start | bytes 3145728 | tf_op jit(solution)/shard_map/all_to_all | solution.py:21
  21.2 134.5 %all-reduce.5.cloned.1.call-start = ((), (), s32[]{:S(2)}) async-start(), calls=%async_computation.25 | async-start | bytes 6291456 | tf_op jit(solution)/shard_map/psum | solution.py:31
  61.8 182.4 %all-reduce.7.cloned.1.call-start = ((), (), s32[]{:S(2)}) async-start(), calls=%async_computation.26 | async-start | bytes 6291456 | tf_op jit(solution)/shard_map/psum | solution.py:31
  155.7 1.3 copy-start
  157.0 87.1 %copy-start.1 = (f32[384]{0:T(512)S(1)}, f32[384]{0:T(512)}, u32[]{:S(2)}) copy-start(f32[384]{0:T(512)} %param.5) | copy-start | bytes 4612
  272.4 16.4 %all-to-all-start.1 = ((f32[32,1,26]{2,1,0:T(1,128)}), f32[32,1,26]{2,1,0:T(1,128)S(1)}, u32[]{:S(2)}, u32[]{:S(2)}) async-start(f32[32,1,26]{2,1,0:T(1,128)} %broadcast_in_dim.171), calls=%async_computation.1 | async-start | bytes 32768 | tf_op jit(solution)/shard_map/all_to_all | solution.py:21
  293.9 22.2 %all-to-all-start.2 = ((f32[32,1,768]{2,1,0:T(1,128)}), f32[32,1,768]{2,1,0:T(1,128)S(1)}, u32[]{:S(2)}, u32[]{:S(2)}) async-start(f32[32,1,768]{2,1,0:T(1,128)} %broadcast_in_dim.172), calls=%async_computation.2 | async-start | bytes 196608 | tf_op jit(solution)/shard_map/all_to_all | solution.py:21
  333.8 18.0 %all-to-all-start.3 = ((f32[32,1,10]{2,1,0:T(1,128)}), f32[32,1,10]{2,1,0:T(1,128)S(1)}, u32[]{:S(2)}, u32[]{:S(2)}) async-start(f32[32,1,10]{2,1,0:T(1,128)} %broadcast_in_dim.173), calls=%async_computation.3 | async-start | bytes 32768 | tf_op jit(solution)/shard_map/all_to_all | solution.py:21
  355.0 20.1 %all-to-all-start.4 = ((f32[32,1,26]{2,1,0:T(1,128)}), f32[32,1,26]{2,1,0:T(1,128)S(1)}, u32[]{:S(2)}, u32[]{:S(2)}) async-start(f32[32,1,26]{2,1,0:T(1,128)} %broadcast_in_dim.174), calls=%async_computation.4 | async-start | bytes 32768 | tf_op jit(solution)/shard_map/all_to_all | solution.py:21
  380.1 18.8 %all-to-all-start.5 = ((f32[32,1,768]{2,1,0:T(1,128)}), f32[32,1,768]{2,1,0:T(1,128)S(1)}, u32[]{:S(2)}, u32[]{:S(2)}) async-start(f32[32,1,768]{2,1,0:T(1,128)} %broadcast_in_dim.175), calls=%async_computation.5 | async-start | bytes 196608 | tf_op jit(solution)/shard_map/all_to_all | solution.py:21
  418.3 12.4 %all-to-all-start.6 = ((f32[32,1,10]{2,1,0:T(1,128)}), f32[32,1,10]{2,1,0:T(1,128)S(1)}, u32[]{:S(2)}, u32[]{:S(2)}) async-start(f32[32,1,10]{2,1,0:T(1,128)} %broadcast_in_dim.176), calls=%async_computation.6 | async-start | bytes 32768 | tf_op jit(solution)/shard_map/all_to_all | solution.py:21
  433.8 19.8 %all-to-all-start.7 = ((f32[32,1,26]{2,1,0:T(1,128)}), f32[32,1,26]{2,1,0:T(1,128)S(1)}, u32[]{:S(2)}, u32[]{:S(2)}) async-start(f32[32,1,26]{2,1,0:T(1,128)} %broadcast_in_dim.177), calls=%async_computation.7 | async-start | bytes 32768 | tf_op jit(solution)/shard_map/all_to_all | solution.py:21
  458.9 18.6 %all-to-all-start.8 = ((f32[32,1,768]{2,1,0:T(1,128)}), f32[32,1,768]{2,1,0:T(1,128)S(1)}, u32[]{:S(2)}, u32[]{:S(2)}) async-start(f32[32,1,768]{2,1,0:T(1,128)} %broadcast_in_dim.178), calls=%async_computation.8 | async-start | bytes 196608 | tf_op jit(solution)/shard_map/all_to_all | solution.py:21
  496.8 12.4 %all-to-all-start.9 = ((f32[32,1,10]{2,1,0:T(1,128)}), f32[32,1,10]{2,1,0:T(1,128)S(1)}, u32[]{:S(2)}, u32[]{:S(2)}) async-start(f32[32,1,10]{2,1,0:T(1,128)} %broadcast_in_dim.179), calls=%async_computation.9 | async-start | bytes 32768 | tf_op jit(solution)/shard_map/all_to_all | solution.py:21
  512.4 19.8 %all-to-all-start.10 = ((f32[32,1,26]{2,1,0:T(1,128)}), f32[32,1,26]{2,1,0:T(1,128)S(1)}, u32[]{:S(2)}, u32[]{:S(2)}) async-start(f32[32,1,26]{2,1,0:T(1,128)} %broadcast_in_dim.180), calls=%async_computation.10 | async-start | bytes 32768 | tf_op jit(solution)/shard_map/all_to_all | solution.py:21
  537.4 18.6 %all-to-all-start.11 = ((f32[32,1,768]{2,1,0:T(1,128)}), f32[32,1,768]{2,1,0:T(1,128)S(1)}, u32[]{:S(2)}, u32[]{:S(2)}) async-start(f32[32,1,768]{2,1,0:T(1,128)} %broadcast_in_dim.181), calls=%async_computation.11 | async-start | bytes 196608 | tf_op jit(solution)/shard_map/all_to_all | solution.py:21
  575.4 12.4 %all-to-all-start.12 = ((f32[32,1,10]{2,1,0:T(1,128)}), f32[32,1,10]{2,1,0:T(1,128)S(1)}, u32[]{:S(2)}, u32[]{:S(2)}) async-start(f32[32,1,10]{2,1,0:T(1,128)} %broadcast_in_dim.182), calls=%async_computation.12 | async-start | bytes 32768 | tf_op jit(solution)/shard_map/all_to_all | solution.py:21
  590.9 19.8 %all-to-all-start.13 = ((f32[32,1,26]{2,1,0:T(1,128)}), f32[32,1,26]{2,1,0:T(1,128)S(1)}, u32[]{:S(2)}, u32[]{:S(2)}) async-start(f32[32,1,26]{2,1,0:T(1,128)} %broadcast_in_dim.183), calls=%async_computation.13 | async-start | bytes 32768 | tf_op jit(solution)/shard_map/all_to_all | solution.py:21
  615.9 18.6 %all-to-all-start.14 = ((f32[32,1,768]{2,1,0:T(1,128)}), f32[32,1,768]{2,1,0:T(1,128)S(1)}, u32[]{:S(2)}, u32[]{:S(2)}) async-start(f32[32,1,768]{2,1,0:T(1,128)} %broadcast_in_dim.184), calls=%async_computation.14 | async-start | bytes 196608 | tf_op jit(solution)/shard_map/all_to_all | solution.py:21
  653.8 12.4 %all-to-all-start.15 = ((f32[32,1,10]{2,1,0:T(1,128)}), f32[32,1,10]{2,1,0:T(1,128)S(1)}, u32[]{:S(2)}, u32[]{:S(2)}) async-start(f32[32,1,10]{2,1,0:T(1,128)} %broadcast_in_dim.185), calls=%async_computation.15 | async-start | bytes 32768 | tf_op jit(solution)/shard_map/all_to_all | solution.py:21
  669.4 20.0 %all-to-all-start.16 = ((f32[32,1,26]{2,1,0:T(1,128)}), f32[32,1,26]{2,1,0:T(1,128)S(1)}, u32[]{:S(2)}, u32[]{:S(2)}) async-start(f32[32,1,26]{2,1,0:T(1,128)} %broadcast_in_dim.186), calls=%async_computation.16 | async-start | bytes 32768 | tf_op jit(solution)/shard_map/all_to_all | solution.py:21
  694.5 18.6 %all-to-all-start.17 = ((f32[32,1,768]{2,1,0:T(1,128)}), f32[32,1,768]{2,1,0:T(1,128)S(1)}, u32[]{:S(2)}, u32[]{:S(2)}) async-start(f32[32,1,768]{2,1,0:T(1,128)} %broadcast_in_dim.187), calls=%async_computation.17 | async-start | bytes 196608 | tf_op jit(solution)/shard_map/all_to_all | solution.py:21
  732.4 12.4 %all-to-all-start.18 = ((f32[32,1,10]{2,1,0:T(1,128)}), f32[32,1,10]{2,1,0:T(1,128)S(1)}, u32[]{:S(2)}, u32[]{:S(2)}) async-start(f32[32,1,10]{2,1,0:T(1,128)} %broadcast_in_dim.188), calls=%async_computation.18 | async-start | bytes 32768 | tf_op jit(solution)/shard_map/all_to_all | solution.py:21
  748.0 19.8 %all-to-all-start.19 = ((f32[32,1,26]{2,1,0:T(1,128)}), f32[32,1,26]{2,1,0:T(1,128)S(1)}, u32[]{:S(2)}, u32[]{:S(2)}) async-start(f32[32,1,26]{2,1,0:T(1,128)} %broadcast_in_dim.189), calls=%async_computation.19 | async-start | bytes 32768 | tf_op jit(solution)/shard_map/all_to_all | solution.py:21
  773.0 18.6 %all-to-all-start.20 = ((f32[32,1,768]{2,1,0:T(1,128)}), f32[32,1,768]{2,1,0:T(1,128)S(1)}, u32[]{:S(2)}, u32[]{:S(2)}) async-start(f32[32,1,768]{2,1,0:T(1,128)} %broadcast_in_dim.190), calls=%async_computation.20 | async-start | bytes 196608 | tf_op jit(solution)/shard_map/all_to_all | solution.py:21
  810.9 12.4 %all-to-all-start.21 = ((f32[32,1,10]{2,1,0:T(1,128)}), f32[32,1,10]{2,1,0:T(1,128)S(1)}, u32[]{:S(2)}, u32[]{:S(2)}) async-start(f32[32,1,10]{2,1,0:T(1,128)} %broadcast_in_dim.191), calls=%async_computation.21 | async-start | bytes 32768 | tf_op jit(solution)/shard_map/all_to_all | solution.py:21
  826.6 12.5 %all-to-all-start.22 = ((f32[32,1,26]{2,1,0:T(1,128)}), f32[32,1,26]{2,1,0:T(1,128)S(1)}, u32[]{:S(2)}, u32[]{:S(2)}) async-start(f32[32,1,26]{2,1,0:T(1,128)} %broadcast_in_dim.192), calls=%async_computation.22 | async-start | bytes 32768 | tf_op jit(solution)/shard_map/all_to_all | solution.py:21
  844.4 13.0 %all-to-all-start.23 = ((f32[32,1,768]{2,1,0:T(1,128)}), f32[32,1,768]{2,1,0:T(1,128)S(1)}, u32[]{:S(2)}, u32[]{:S(2)}) async-start(f32[32,1,768]{2,1,0:T(1,128)} %broadcast_in_dim.193), calls=%async_computation.23 | async-start | bytes 196608 | tf_op jit(solution)/shard_map/all_to_all | solution.py:21
  877.7 13.5 %all-to-all-start.24 = ((f32[32,1,10]{2,1,0:T(1,128)}), f32[32,1,10]{2,1,0:T(1,128)S(1)}, u32[]{:S(2)}, u32[]{:S(2)}) async-start(f32[32,1,10]{2,1,0:T(1,128)} %broadcast_in_dim.194), calls=%async_computation.24 | async-start | bytes 32768 | tf_op jit(solution)/shard_map/all_to_all | solution.py:21
Sparse Core Ops, SparseCore 0:
  61.9 93.7 all-reduce.4
  158.1 85.9 all-reduce.6
where the time goes:
time: 901 us; the launch traced here: 899 us
  waiting for transfers between devices  356 us (40%)
  blocking collectives  268 us (30%)
  starting transfers between devices  149 us (17%)
  between operations  36.2 us (4%)
  local copies, waits for them, and re-layouts  33.9 us (4%)
  other arithmetic  30.2 us (3%)
  matrix products  25.4 us (3%)
    all_gather x16, blocking collectives, picked(): lax.all_gather(value, axis)  268 us
    psum x2, waiting for transfers between devices, spread(): value = lax.psum(value, axis)  179 us
    all_to_all x25, waiting for transfers between devices, sent_to_all(): return lax.all_to_all(copies, axis, split_axis=0, concat_axis=0, tiled=True)  177 us
    all_to_all x25, starting transfers between devices, sent_to_all(): return lax.all_to_all(copies, axis, split_axis=0, concat_axis=0, tiled=True)  149 us
  transfers between devices with their start and end apart: 27, of which 20 were waited for; matrix products, arithmetic and copies ran while one was open for 2% of the time, Pallas kernels for 0%

commit v1 on v0

--- a/solution.py
+++ b/solution.py
@@ -28,7 +28,8 @@
 def spread(value, axes, root):
     value = jnp.where(lax.axis_index(axes) == root, value, jnp.zeros_like(value))
     for axis in axes:
-        value = lax.psum(value, axis)
+        parts = lax.all_gather(value, axis)
+        value = jnp.sum(parts, axis=0)
     return value
 
 

time: 901 us -> 1140 us (1.27)
  waiting for transfers between devices: 356 us -> 570 us
  other arithmetic: 30.2 us -> 54.7 us
    all_gather x0 -> x4, waiting for transfers between devices: none -> 392 us  [spread(): parts = lax.all_gather(value, axis)]
    psum x2 -> x0, waiting for transfers between devices: 179 us -> none  [spread(): value = lax.psum(value, axis)]
    reduce_sum x0 -> x4, other arithmetic: none -> 24.4 us  [spread(): value = jnp.sum(parts, axis=0)]
  transfers between devices with their start and end apart: 27 -> 29, of which waited for: 20 -> 22; matrix products, arithmetic and copies ran while one was open for 2% -> 3% of each run, Pallas kernels for 0% -> 0%
where the time goes in v1:
time: 1140 us
  waiting for transfers between devices  570 us (50%)
  blocking collectives  269 us (24%)
  starting transfers between devices  150 us (13%)
  other arithmetic  54.7 us (5%)
  between operations  36.1 us (3%)
  local copies, waits for them, and re-layouts  33.9 us (3%)
  matrix products  25.4 us (2%)
    all_gather x4, waiting for transfers between devices, spread(): parts = lax.all_gather(value, axis)  392 us
    all_gather x16, blocking collectives, picked(): lax.all_gather(value, axis)  269 us
    all_to_all x25, waiting for transfers between devices, sent_to_all(): return lax.all_to_all(copies, axis, split_axis=0, concat_axis=0, tiled=True)  177 us
    all_to_all x25, starting transfers between devices, sent_to_all(): return lax.all_to_all(copies, axis, split_axis=0, concat_axis=0, tiled=True)  149 us
    reduce_sum x4, other arithmetic, spread(): value = jnp.sum(parts, axis=0)  24.4 us
  transfers between devices with their start and end apart: 29, of which 22 were waited for; matrix products, arithmetic and copies ran while one was open for 3% of the time, Pallas kernels for 0%

profile of v1, /device:TPU:1, one launch (start us, length us, event | category | flops | bytes accessed | tf_op | source)
XLA Modules:
  0.0 1138.3 jit_solution(15149874602265984991)
XLA Ops:
  9.4 11.8 %all-to-all-start = ((f32[16,24,1024]{2,1,0:T(8,128)}), f32[16,24,1024]{2,1,0:T(8,128)S(1)}, u32[]{:S(2)}, u32[]{:S(2)}) async-start(f32[16,24,1024]{2,1,0:T(8,128)} %broadcast_in_dim.166), calls=%async_computation | async-start | bytes 3145728 | tf_op jit(solution)/shard_map/all_to_all | solution.py:21
  21.3 38.5 %all-to-all-done = f32[16,24,1024]{2,1,0:T(8,128)S(1)} async-done(((f32[16,24,1024]{2,1,0:T(8,128)}), f32[16,24,1024]{2,1,0:T(8,128)S(1)}, u32[]{:S(2)}, u32[]{:S(2)}) %all-to-all-start) | async-done | bytes 1572896 | tf_op jit(solution)/shard_map/all_to_all | solution.py:21
  62.7 132.7 %all-gather.31.cloned.1.call-done = f32[8,384,1024]{2,1,0:T(8,128)} async-done(((f32[1,384,1024]{2,1,0:T(8,128)}), f32[8,384,1024]{2,1,0:T(8,128)}) %all-gather.31.cloned.1.call-update) | async-done | bytes 12582928 | tf_op jit(solution)/shard_map/all_gather | solution.py:31
  195.4 7.4 reduce_sum.396
  203.3 128.9 %all-gather.33.cloned.1.call-done = f32[8,384,1024]{2,1,0:T(8,128)} async-done(((f32[1,384,1024]{2,1,0:T(8,128)}), f32[8,384,1024]{2,1,0:T(8,128)}) %all-gather.33.cloned.1.call-update) | async-done | bytes 12582928 | tf_op jit(solution)/shard_map/all_gather | solution.py:31
  332.3 7.4 reduce_sum.398
  343.1 61.3 %all-gather.35.cloned.1.call-done = f32[1536,1024]{1,0:T(8,128)} async-done(((f32[384,1024]{1,0:T(8,128)}), f32[1536,1024]{1,0:T(8,128)}) %all-gather.35.cloned.1.call-update) | async-done | bytes 6291472 | tf_op jit(solution)/shard_map/all_gather | solution.py:31
  404.4 4.8 reduce_sum.397
  409.2 68.9 %all-gather.37.cloned.1.call-done = f32[1536,1024]{1,0:T(8,128)} async-done(((f32[384,1024]{1,0:T(8,128)}), f32[1536,1024]{1,0:T(8,128)}) %all-gather.37.cloned.1.call-update) | async-done | bytes 6291472 | tf_op jit(solution)/shard_map/all_gather | solution.py:31
  478.1 4.9 reduce_sum.399
  482.9 7.3 fusion.13
  490.2 18.8 %all-gather.2 = f32[6144,1]{0,1:T(1,128)S(1)} all-gather(f32[384,1]{0,1:T(1,128)S(1)} %get-tuple-element.89), channel_id=4, replica_groups=mesh['row_0'=8,'row_1'=4,'col'=16] {'col'}, dimensions={0}, use_global_device_ids=true | all-gather | bytes 26112 | tf_op jit(solution)/shard_map/all_gather | solution.py:37
  511.2 8.7 all-to-all-start.1
  519.9 8.5 all-to-all-done.1
  533.5 3.9 all-to-all-start.2
  537.3 16.2 %all-gather.3 = f32[6144,1]{0,1:T(1,128)S(1)} all-gather(f32[384,1]{0,1:T(1,128)S(1)} %get-tuple-element.88), channel_id=5, replica_groups=mesh['row_0'=8,'row_1'=4,'col'=16] {'col'}, dimensions={0}, use_global_device_ids=true | all-gather | bytes 26112 | tf_op jit(solution)/shard_map/all_gather | solution.py:37
  555.7 15.8 %all-gather.18 = f32[16,1,768]{2,1,0:T(1,128)S(1)} all-gather(f32[1,1,768]{2,1,0:T(1,128)S(1)} %reshape.435), channel_id=6, replica_groups=mesh['row_0'=8,'row_1'=4,'col'=16] {'col'}, dimensions={0}, use_global_device_ids=true | all-gather | bytes 52224 | tf_op jit(solution)/shard_map/all_gather | solution.py:37
  573.6 9.5 all-to-all-start.3
  583.1 8.5 all-to-all-done.3
  594.8 3.8 all-to-all-start.4
  598.6 16.2 %all-gather.5 = f32[6144,1]{0,1:T(1,128)S(1)} all-gather(f32[384,1]{0,1:T(1,128)S(1)} %get-tuple-element.87), channel_id=7, replica_groups=mesh['row_0'=8,'row_1'=4,'col'=16] {'col'}, dimensions={0}, use_global_device_ids=true | all-gather | bytes 26112 | tf_op jit(solution)/shard_map/all_gather | solution.py:37
  619.9 9.5 all-to-all-start.5
  629.9 8.6 all-to-all-done.5
  638.6 17.2 %all-gather.19 = f32[16,1,768]{2,1,0:T(1,128)S(1)} all-gather(f32[1,1,768]{2,1,0:T(1,128)S(1)} %reshape.437), channel_id=8, replica_groups=mesh['row_0'=8,'row_1'=4,'col'=16] {'col'}, dimensions={0}, use_global_device_ids=true | all-gather | bytes 52224 | tf_op jit(solution)/shard_map/all_gather | solution.py:37
  657.9 3.8 all-to-all-start.6
  661.7 8.5 all-to-all-done.6
  673.4 3.8 all-to-all-start.7
  677.3 15.9 %all-gather.7 = f32[6144,1]{0,1:T(1,128)S(1)} all-gather(f32[384,1]{0,1:T(1,128)S(1)} %get-tuple-element.86), channel_id=9, replica_groups=mesh['row_0'=8,'row_1'=4,'col'=16] {'col'}, dimensions={0}, use_global_device_ids=true | all-gather | bytes 26112 | tf_op jit(solution)/shard_map/all_gather | solution.py:37
  698.5 9.5 all-to-all-start.8
  708.4 8.6 all-to-all-done.8
  717.1 17.2 %all-gather.20 = f32[16,1,768]{2,1,0:T(1,128)S(1)} all-gather(f32[1,1,768]{2,1,0:T(1,128)S(1)} %reshape.439), channel_id=10, replica_groups=mesh['row_0'=8,'row_1'=4,'col'=16] {'col'}, dimensions={0}, use_global_device_ids=true | all-gather | bytes 52224 | tf_op jit(solution)/shard_map/all_gather | solution.py:37
  736.4 3.8 all-to-all-start.9
  740.3 8.5 all-to-all-done.9
  752.0 3.8 all-to-all-start.10
  755.8 15.9 %all-gather.9 = f32[6144,1]{0,1:T(1,128)S(1)} all-gather(f32[384,1]{0,1:T(1,128)S(1)} %get-tuple-element.85), channel_id=11, replica_groups=mesh['row_0'=8,'row_1'=4,'col'=16] {'col'}, dimensions={0}, use_global_device_ids=true | all-gather | bytes 26112 | tf_op jit(solution)/shard_map/all_gather | solution.py:37
  777.0 9.5 all-to-all-start.11
  787.0 8.6 all-to-all-done.11
  795.7 17.2 %all-gather.21 = f32[16,1,768]{2,1,0:T(1,128)S(1)} all-gather(f32[1,1,768]{2,1,0:T(1,128)S(1)} %reshape.441), channel_id=12, replica_groups=mesh['row_0'=8,'row_1'=4,'col'=16] {'col'}, dimensions={0}, use_global_device_ids=true | all-gather | bytes 52224 | tf_op jit(solution)/shard_map/all_gather | solution.py:37
  818.8 8.5 all-to-all-done.12
  834.4 16.2 %all-gather.11 = f32[6144,1]{0,1:T(1,128)S(1)} all-gather(f32[384,1]{0,1:T(1,128)S(1)} %get-tuple-element.84), channel_id=13, replica_groups=mesh['row_0'=8,'row_1'=4,'col'=16] {'col'}, dimensions={0}, use_global_device_ids=true | all-gather | bytes 26112 | tf_op jit(solution)/shard_map/all_gather | solution.py:37
  855.7 9.5 all-to-all-start.14
  865.6 8.6 all-to-all-done.14
  874.3 17.2 %all-gather.22 = f32[16,1,768]{2,1,0:T(1,128)S(1)} all-gather(f32[1,1,768]{2,1,0:T(1,128)S(1)} %reshape.443), channel_id=14, replica_groups=mesh['row_0'=8,'row_1'=4,'col'=16] {'col'}, dimensions={0}, use_global_device_ids=true | all-gather | bytes 52224 | tf_op jit(solution)/shard_map/all_gather | solution.py:37
  893.6 3.8 all-to-all-start.15
  897.5 8.5 all-to-all-done.15
  913.0 15.9 %all-gather.13 = f32[6144,1]{0,1:T(1,128)S(1)} all-gather(f32[384,1]{0,1:T(1,128)S(1)} %get-tuple-element.83), channel_id=15, replica_groups=mesh['row_0'=8,'row_1'=4,'col'=16] {'col'}, dimensions={0}, use_global_device_ids=true | all-gather | bytes 26112 | tf_op jit(solution)/shard_map/all_gather | solution.py:37
  934.1 9.5 all-to-all-start.17
  944.1 8.6 all-to-all-done.17
  952.7 17.2 %all-gather.23 = f32[16,1,768]{2,1,0:T(1,128)S(1)} all-gather(f32[1,1,768]{2,1,0:T(1,128)S(1)} %reshape.445), channel_id=16, replica_groups=mesh['row_0'=8,'row_1'=4,'col'=16] {'col'}, dimensions={0}, use_global_device_ids=true | all-gather | bytes 52224 | tf_op jit(solution)/shard_map/all_gather | solution.py:37
  972.0 3.8 all-to-all-start.18
  975.9 8.5 all-to-all-done.18
  991.5 15.9 %all-gather.15 = f32[6144,1]{0,1:T(1,128)S(1)} all-gather(f32[384,1]{0,1:T(1,128)S(1)} %get-tuple-element.82), channel_id=17, replica_groups=mesh['row_0'=8,'row_1'=4,'col'=16] {'col'}, dimensions={0}, use_global_device_ids=true | all-gather | bytes 26112 | tf_op jit(solution)/shard_map/all_gather | solution.py:37
  1012.5 9.5 all-to-all-start.20
  1022.5 8.6 all-to-all-done.20
  1031.2 17.2 %all-gather.24 = f32[16,1,768]{2,1,0:T(1,128)S(1)} all-gather(f32[1,1,768]{2,1,0:T(1,128)S(1)} %reshape.447), channel_id=18, replica_groups=mesh['row_0'=8,'row_1'=4,'col'=16] {'col'}, dimensions={0}, use_global_device_ids=true | all-gather | bytes 52224 | tf_op jit(solution)/shard_map/all_gather | solution.py:37
  1050.5 3.8 all-to-all-start.21
  1054.4 8.5 all-to-all-done.21
  1066.1 3.8 all-to-all-start.22
  1071.4 7.2 all-to-all-done.22
  1084.0 3.9 all-to-all-start.23
  1087.9 4.9 stack.39
  1097.1 18.1 %all-gather.25 = f32[16,1,768]{2,1,0:T(1,128)S(1)} all-gather(f32[1,1,768]{2,1,0:T(1,128)S(1)} %reshape.449), channel_id=19, replica_groups=mesh['row_0'=8,'row_1'=4,'col'=16] {'col'}, dimensions={0}, use_global_device_ids=true | all-gather | bytes 52224 | tf_op jit(solution)/shard_map/all_gather | solution.py:37
  1117.2 4.9 all-to-all-start.24
  1122.7 8.1 all-to-all-done.24
  (273 shorter events, 97.6 us)
Async XLA Ops:
  9.4 50.3 %all-to-all-start = ((f32[16,24,1024]{2,1,0:T(8,128)}), f32[16,24,1024]{2,1,0:T(8,128)S(1)}, u32[]{:S(2)}, u32[]{:S(2)}) async-start(f32[16,24,1024]{2,1,0:T(8,128)} %broadcast_in_dim.166), calls=%async_computation | async-start | bytes 3145728 | tf_op jit(solution)/shard_map/all_to_all | solution.py:21
  21.2 174.2 %all-gather.31.cloned.1.call-start = ((), (), s32[]{:S(2)}) async-start(), calls=%async_computation.25 | async-start | bytes 14155776 | tf_op jit(solution)/shard_map/all_gather | solution.py:31
  61.9 270.4 %all-gather.33.cloned.1.call-start = ((), (), s32[]{:S(2)}) async-start(), calls=%async_computation.26 | async-start | bytes 14155776 | tf_op jit(solution)/shard_map/all_gather | solution.py:31
  62.7 341.7 %all-gather.35.cloned.1.call-start = ((), (), s32[]{:S(2)}) async-start(), calls=%async_computation.27 | async-start | bytes 7864320 | tf_op jit(solution)/shard_map/all_gather | solution.py:31
  202.8 275.2 %all-gather.37.cloned.1.call-start = ((), (), s32[]{:S(2)}) async-start(), calls=%async_computation.28 | async-start | bytes 7864320 | tf_op jit(solution)/shard_map/all_gather | solution.py:31
  339.7 1.3 copy-start
  478.1 4.9 copy-start.1
  511.2 17.2 %all-to-all-start.1 = ((f32[32,1,26]{2,1,0:T(1,128)}), f32[32,1,26]{2,1,0:T(1,128)S(1)}, u32[]{:S(2)}, u32[]{:S(2)}) async-start(f32[32,1,26]{2,1,0:T(1,128)} %broadcast_in_dim.171), calls=%async_computation.1 | async-start | bytes 32768 | tf_op jit(solution)/shard_map/all_to_all | solution.py:21
  533.5 22.2 %all-to-all-start.2 = ((f32[32,1,768]{2,1,0:T(1,128)}), f32[32,1,768]{2,1,0:T(1,128)S(1)}, u32[]{:S(2)}, u32[]{:S(2)}) async-start(f32[32,1,768]{2,1,0:T(1,128)} %broadcast_in_dim.172), calls=%async_computation.2 | async-start | bytes 196608 | tf_op jit(solution)/shard_map/all_to_all | solution.py:21
  573.6 18.0 %all-to-all-start.3 = ((f32[32,1,10]{2,1,0:T(1,128)}), f32[32,1,10]{2,1,0:T(1,128)S(1)}, u32[]{:S(2)}, u32[]{:S(2)}) async-start(f32[32,1,10]{2,1,0:T(1,128)} %broadcast_in_dim.173), calls=%async_computation.3 | async-start | bytes 32768 | tf_op jit(solution)/shard_map/all_to_all | solution.py:21
  594.8 20.0 %all-to-all-start.4 = ((f32[32,1,26]{2,1,0:T(1,128)}), f32[32,1,26]{2,1,0:T(1,128)S(1)}, u32[]{:S(2)}, u32[]{:S(2)}) async-start(f32[32,1,26]{2,1,0:T(1,128)} %broadcast_in_dim.174), calls=%async_computation.4 | async-start | bytes 32768 | tf_op jit(solution)/shard_map/all_to_all | solution.py:21
  619.9 18.6 %all-to-all-start.5 = ((f32[32,1,768]{2,1,0:T(1,128)}), f32[32,1,768]{2,1,0:T(1,128)S(1)}, u32[]{:S(2)}, u32[]{:S(2)}) async-start(f32[32,1,768]{2,1,0:T(1,128)} %broadcast_in_dim.175), calls=%async_computation.5 | async-start | bytes 196608 | tf_op jit(solution)/shard_map/all_to_all | solution.py:21
  657.9 12.4 %all-to-all-start.6 = ((f32[32,1,10]{2,1,0:T(1,128)}), f32[32,1,10]{2,1,0:T(1,128)S(1)}, u32[]{:S(2)}, u32[]{:S(2)}) async-start(f32[32,1,10]{2,1,0:T(1,128)} %broadcast_in_dim.176), calls=%async_computation.6 | async-start | bytes 32768 | tf_op jit(solution)/shard_map/all_to_all | solution.py:21
  673.4 19.8 %all-to-all-start.7 = ((f32[32,1,26]{2,1,0:T(1,128)}), f32[32,1,26]{2,1,0:T(1,128)S(1)}, u32[]{:S(2)}, u32[]{:S(2)}) async-start(f32[32,1,26]{2,1,0:T(1,128)} %broadcast_in_dim.177), calls=%async_computation.7 | async-start | bytes 32768 | tf_op jit(solution)/shard_map/all_to_all | solution.py:21
  698.5 18.6 %all-to-all-start.8 = ((f32[32,1,768]{2,1,0:T(1,128)}), f32[32,1,768]{2,1,0:T(1,128)S(1)}, u32[]{:S(2)}, u32[]{:S(2)}) async-start(f32[32,1,768]{2,1,0:T(1,128)} %broadcast_in_dim.178), calls=%async_computation.8 | async-start | bytes 196608 | tf_op jit(solution)/shard_map/all_to_all | solution.py:21
  736.4 12.4 %all-to-all-start.9 = ((f32[32,1,10]{2,1,0:T(1,128)}), f32[32,1,10]{2,1,0:T(1,128)S(1)}, u32[]{:S(2)}, u32[]{:S(2)}) async-start(f32[32,1,10]{2,1,0:T(1,128)} %broadcast_in_dim.179), calls=%async_computation.9 | async-start | bytes 32768 | tf_op jit(solution)/shard_map/all_to_all | solution.py:21
  752.0 19.8 %all-to-all-start.10 = ((f32[32,1,26]{2,1,0:T(1,128)}), f32[32,1,26]{2,1,0:T(1,128)S(1)}, u32[]{:S(2)}, u32[]{:S(2)}) async-start(f32[32,1,26]{2,1,0:T(1,128)} %broadcast_in_dim.180), calls=%async_computation.10 | async-start | bytes 32768 | tf_op jit(solution)/shard_map/all_to_all | solution.py:21
  777.0 18.6 %all-to-all-start.11 = ((f32[32,1,768]{2,1,0:T(1,128)}), f32[32,1,768]{2,1,0:T(1,128)S(1)}, u32[]{:S(2)}, u32[]{:S(2)}) async-start(f32[32,1,768]{2,1,0:T(1,128)} %broadcast_in_dim.181), calls=%async_computation.11 | async-start | bytes 196608 | tf_op jit(solution)/shard_map/all_to_all | solution.py:21
  815.0 12.4 %all-to-all-start.12 = ((f32[32,1,10]{2,1,0:T(1,128)}), f32[32,1,10]{2,1,0:T(1,128)S(1)}, u32[]{:S(2)}, u32[]{:S(2)}) async-start(f32[32,1,10]{2,1,0:T(1,128)} %broadcast_in_dim.182), calls=%async_computation.12 | async-start | bytes 32768 | tf_op jit(solution)/shard_map/all_to_all | solution.py:21
  830.5 20.0 %all-to-all-start.13 = ((f32[32,1,26]{2,1,0:T(1,128)}), f32[32,1,26]{2,1,0:T(1,128)S(1)}, u32[]{:S(2)}, u32[]{:S(2)}) async-start(f32[32,1,26]{2,1,0:T(1,128)} %broadcast_in_dim.183), calls=%async_computation.13 | async-start | bytes 32768 | tf_op jit(solution)/shard_map/all_to_all | solution.py:21
  855.7 18.6 %all-to-all-start.14 = ((f32[32,1,768]{2,1,0:T(1,128)}), f32[32,1,768]{2,1,0:T(1,128)S(1)}, u32[]{:S(2)}, u32[]{:S(2)}) async-start(f32[32,1,768]{2,1,0:T(1,128)} %broadcast_in_dim.184), calls=%async_computation.14 | async-start | bytes 196608 | tf_op jit(solution)/shard_map/all_to_all | solution.py:21
  893.6 12.4 %all-to-all-start.15 = ((f32[32,1,10]{2,1,0:T(1,128)}), f32[32,1,10]{2,1,0:T(1,128)S(1)}, u32[]{:S(2)}, u32[]{:S(2)}) async-start(f32[32,1,10]{2,1,0:T(1,128)} %broadcast_in_dim.185), calls=%async_computation.15 | async-start | bytes 32768 | tf_op jit(solution)/shard_map/all_to_all | solution.py:21
  909.2 19.8 %all-to-all-start.16 = ((f32[32,1,26]{2,1,0:T(1,128)}), f32[32,1,26]{2,1,0:T(1,128)S(1)}, u32[]{:S(2)}, u32[]{:S(2)}) async-start(f32[32,1,26]{2,1,0:T(1,128)} %broadcast_in_dim.186), calls=%async_computation.16 | async-start | bytes 32768 | tf_op jit(solution)/shard_map/all_to_all | solution.py:21
  934.1 18.6 %all-to-all-start.17 = ((f32[32,1,768]{2,1,0:T(1,128)}), f32[32,1,768]{2,1,0:T(1,128)S(1)}, u32[]{:S(2)}, u32[]{:S(2)}) async-start(f32[32,1,768]{2,1,0:T(1,128)} %broadcast_in_dim.187), calls=%async_computation.17 | async-start | bytes 196608 | tf_op jit(solution)/shard_map/all_to_all | solution.py:21
  972.0 12.4 %all-to-all-start.18 = ((f32[32,1,10]{2,1,0:T(1,128)}), f32[32,1,10]{2,1,0:T(1,128)S(1)}, u32[]{:S(2)}, u32[]{:S(2)}) async-start(f32[32,1,10]{2,1,0:T(1,128)} %broadcast_in_dim.188), calls=%async_computation.18 | async-start | bytes 32768 | tf_op jit(solution)/shard_map/all_to_all | solution.py:21
  987.6 19.8 %all-to-all-start.19 = ((f32[32,1,26]{2,1,0:T(1,128)}), f32[32,1,26]{2,1,0:T(1,128)S(1)}, u32[]{:S(2)}, u32[]{:S(2)}) async-start(f32[32,1,26]{2,1,0:T(1,128)} %broadcast_in_dim.189), calls=%async_computation.19 | async-start | bytes 32768 | tf_op jit(solution)/shard_map/all_to_all | solution.py:21
  1012.5 18.6 %all-to-all-start.20 = ((f32[32,1,768]{2,1,0:T(1,128)}), f32[32,1,768]{2,1,0:T(1,128)S(1)}, u32[]{:S(2)}, u32[]{:S(2)}) async-start(f32[32,1,768]{2,1,0:T(1,128)} %broadcast_in_dim.190), calls=%async_computation.20 | async-start | bytes 196608 | tf_op jit(solution)/shard_map/all_to_all | solution.py:21
  1050.5 12.4 %all-to-all-start.21 = ((f32[32,1,10]{2,1,0:T(1,128)}), f32[32,1,10]{2,1,0:T(1,128)S(1)}, u32[]{:S(2)}, u32[]{:S(2)}) async-start(f32[32,1,10]{2,1,0:T(1,128)} %broadcast_in_dim.191), calls=%async_computation.21 | async-start | bytes 32768 | tf_op jit(solution)/shard_map/all_to_all | solution.py:21
  1066.1 12.5 %all-to-all-start.22 = ((f32[32,1,26]{2,1,0:T(1,128)}), f32[32,1,26]{2,1,0:T(1,128)S(1)}, u32[]{:S(2)}, u32[]{:S(2)}) async-start(f32[32,1,26]{2,1,0:T(1,128)} %broadcast_in_dim.192), calls=%async_computation.22 | async-start | bytes 32768 | tf_op jit(solution)/shard_map/all_to_all | solution.py:21
  1084.0 13.0 %all-to-all-start.23 = ((f32[32,1,768]{2,1,0:T(1,128)}), f32[32,1,768]{2,1,0:T(1,128)S(1)}, u32[]{:S(2)}, u32[]{:S(2)}) async-start(f32[32,1,768]{2,1,0:T(1,128)} %broadcast_in_dim.193), calls=%async_computation.23 | async-start | bytes 196608 | tf_op jit(solution)/shard_map/all_to_all | solution.py:21
  1117.2 13.5 %all-to-all-start.24 = ((f32[32,1,10]{2,1,0:T(1,128)}), f32[32,1,10]{2,1,0:T(1,128)S(1)}, u32[]{:S(2)}, u32[]{:S(2)}) async-start(f32[32,1,10]{2,1,0:T(1,128)} %broadcast_in_dim.194), calls=%async_computation.24 | async-start | bytes 32768 | tf_op jit(solution)/shard_map/all_to_all | solution.py:21
Sparse Core Ops, SparseCore 0:
  62.0 133.3 all-gather.30
  197.5 134.7 all-gather.32
  334.4 69.9 all-gather.34
  406.4 71.6 all-gather.36
